TPU v7x, 32 devices: a whole 2x2x4 slice. The times are simulated.
32 devices in a mesh: seq: 8 (over z, y), opt: 4 (over x, core).
Axes of the slice: x: 2, y: 2, z: 4, core: 2. Of those that a mesh axis runs over, the one named last changes fastest.
Arguments:
- layer_in: bfloat16 [4, 4096, 4096], P('opt', 'seq'), may hold values from -48 to 48, as said below
- ssm_input: bfloat16 [4, 4096, 4096], P('opt', 'seq'), may hold values from -0.119628906 to 0.119628906
- grad_out: bfloat16 [4, 4096, 4096], P('opt', 'seq'), may hold values from -0.59765625 to 0.59765625
- log_decay: float32 [4, 32, 4096], P('opt', None, 'seq'), may hold values from -1 to 0, as said below
- skip_gain: float32 [32], replicated, may hold values from 0.5 to 2
- w_bc: float32 [4096, 256], P(('seq', 'opt')), may hold values from -0.0078125 to 0.0078125
- m_code: bfloat16 [4096, 256], P(('seq', 'opt')), may hold values from -1 to 1
- m_scale: float32 [256], replicated, may hold values from 0.0001 to 0.001
- row_stat: float32 [4096], P(('seq', 'opt')), may hold values from 3e-07 to 3e-06
- col_stat: float32 [256], replicated, may hold values from 3e-07 to 3e-06
Outputs:
- grad_input: bfloat16 [4, 4096, 4096], P('opt', 'seq')
- update: float32 [4096, 256], P(('seq', 'opt'))
- code_next: bfloat16 [4096, 256], P(('seq', 'opt'))
- scale_next: float32 [256], replicated
- row_next: float32 [4096], P(('seq', 'opt'))
- col_next: float32 [256], replicated
Inputs may be any that keep to these rules, and one draw needn't show every extreme that they name: `layer_in`: real-valued rows of order one. `log_decay`: negative log decays.
All inputs are finite; a program needn't handle non-finite values.
Results may differ from a plain program's by a relative error of at most 0.0095.
Values may be sent and summed in bfloat16 or wider, within the bound.
A program may use at most 256 MiB of HBM per device.

v0:
```python
import jax
import jax.numpy as jnp
from jax import lax
from jax.sharding import PartitionSpec as P

D = 4096
BLOCK = 256


beta_one = 0.9
beta_two = 0.95
weight_decay = 0.1
clip_norm = 1.0
tiny_square = 1e-30
adam_floor = 1e-08
peak_floor = 1e-06
norm_floor = 1e-06
highest = lax.Precision.HIGHEST


def carried_in(part, axis, combine, identity, reverse):
    count = lax.axis_size(axis)
    place = lax.axis_index(axis)
    ahead = count - 1 - place if reverse else place
    gathered = jax.tree.map(lambda a: lax.all_gather(a, axis), part)
    state = jax.tree.map(lambda a, e: jnp.zeros_like(a) + jnp.asarray(e, a.dtype), part, identity)

    def one(lap, state):
        source = count - 1 - lap if reverse else lap
        return combine(
            state, jax.tree.map(lambda a: lax.dynamic_index_in_dim(a, source, 0, False), gathered)
        )

    return lax.fori_loop(0, ahead, one, state)


def lower_decays(running):
    length = running.shape[1]
    row_pos = lax.broadcasted_iota(jnp.int32, (length, length), 0)
    col_pos = lax.broadcasted_iota(jnp.int32, (length, length), 1)
    spread = running[:, :, None] - running[:, None, :]
    return jnp.exp(jnp.where((row_pos >= col_pos)[None], spread, -jnp.inf))


def state_adds(feat_blk, cot_blk, b_rows, c_rows, running):
    closing = running[:, -1]
    shrink = jnp.exp(closing[:, None] - running)
    grow = jnp.exp(running)
    forward_add = jnp.einsum(
        "htn,thp->hnp", shrink[:, :, None] * b_rows[None], feat_blk, precision=highest
    )
    backward_add = jnp.einsum(
        "htn,thp->hnp", grow[:, :, None] * c_rows[None], cot_blk, precision=highest
    )
    return (forward_add, backward_add)


def block_terms(halves, feat_blk, cot_blk, b_rows, c_rows, running, state_in, grad_in, skip_gain):
    feat_half, cot_half, b_half, c_half = halves
    closing = running[:, -1]
    decays = lower_decays(running)
    grow = jnp.exp(running)
    shrink = jnp.exp(closing[:, None] - running)
    intersection = jnp.einsum(
        "thp,shp->hts", feat_half, cot_half, preferred_element_type=jnp.float32
    )
    affinity = lax.dot_general(
        b_half, c_half, (((1,), (1,)), ((), ())), preferred_element_type=jnp.float32
    )
    mixing = jnp.sum(decays * jnp.transpose(intersection, (0, 2, 1)), axis=0)
    left_in = jnp.einsum("hnp,thp->htn", state_in, cot_blk, precision=highest)
    grad_cmat = jnp.dot(mixing, b_rows, precision=highest) + jnp.sum(
        grow[:, :, None] * left_in, axis=0
    )
    right_in = jnp.einsum("hnp,thp->htn", grad_in, feat_blk, precision=highest)
    grad_bmat = jnp.dot(mixing.T, c_rows, precision=highest) + jnp.sum(
        shrink[:, :, None] * right_in, axis=0
    )
    weighted = jnp.transpose(decays, (0, 2, 1)) * affinity[None]
    inner = jnp.einsum("hts,shp->thp", weighted, cot_blk, precision=highest)
    outer = jnp.einsum("tn,hnp->thp", b_rows, grad_in, precision=highest) * shrink.T[:, :, None]
    grad_feat = inner + outer + skip_gain[None, :, None] * cot_blk
    return (grad_feat, jnp.concatenate([grad_bmat, grad_cmat], axis=1))


def chain_step(earlier, later):
    return (earlier[0] * later[0], later[0][:, None, None] * earlier[1] + later[1])


def per_device(
    layer_in, ssm_input, grad_out, log_decay, skip_gain, w_bc, m_code, m_scale, row_stat, col_stat
):
    layer_rows = layer_in[0]
    length = layer_rows.shape[0]
    heads = skip_gain.shape[0]
    head_dim = ssm_input.shape[2] // heads
    state_dim = w_bc.shape[1] // 2
    w_half = w_bc.astype(jnp.bfloat16)
    columns = layer_rows
    proj = jnp.dot(
        columns,
        lax.all_gather(w_half, ("seq", "opt"), axis=0, tiled=True),
        preferred_element_type=jnp.float32,
    ).astype(jnp.bfloat16)
    b_bf = proj[:, :state_dim]
    c_bf = proj[:, state_dim:]
    b_all = b_bf.astype(jnp.float32)
    c_all = c_bf.astype(jnp.float32)
    feat_bf = ssm_input[0].reshape(length, heads, head_dim)
    cot_bf = grad_out[0].reshape(length, heads, head_dim)
    feats = feat_bf.astype(jnp.float32)
    cots = cot_bf.astype(jnp.float32)
    logs = log_decay[0]
    count = length // BLOCK
    pieces = []
    halves_list = []
    for number in range(count):
        lower_end = number * BLOCK
        upper_end = lower_end + BLOCK
        running = jnp.cumsum(logs[:, lower_end:upper_end], axis=1)
        pieces.append(
            (
                feats[lower_end:upper_end],
                cots[lower_end:upper_end],
                b_all[lower_end:upper_end],
                c_all[lower_end:upper_end],
                running,
            )
        )
        halves_list.append(
            (
                feat_bf[lower_end:upper_end],
                cot_bf[lower_end:upper_end],
                b_bf[lower_end:upper_end],
                c_bf[lower_end:upper_end],
            )
        )
    zero_state = jnp.zeros((heads, state_dim, head_dim), jnp.float32)
    local_in = [zero_state]
    backward_adds = []
    start_logs = [jnp.zeros((heads,), jnp.float32)]
    for number in range(count):
        feat_blk, cot_blk, b_rows, c_rows, running = pieces[number]
        forward_add, backward_add = state_adds(feat_blk, cot_blk, b_rows, c_rows, running)
        local_in.append(jnp.exp(running[:, -1])[:, None, None] * local_in[number] + forward_add)
        backward_adds.append(backward_add)
        start_logs.append(start_logs[number] + running[:, -1])
    local_out = [zero_state] * count
    after_logs = [jnp.zeros((heads,), jnp.float32)] * count
    carried = zero_state
    after_sum = jnp.zeros((heads,), jnp.float32)
    for number in reversed(range(count)):
        local_out[number] = carried
        after_logs[number] = after_sum
        running = pieces[number][4]
        carried = jnp.exp(running[:, -1])[:, None, None] * carried + backward_adds[number]
        after_sum = after_sum + running[:, -1]
    carry_decay = jnp.exp(start_logs[count])
    identity = (jnp.ones((heads,), jnp.float32), zero_state)
    state_in = carried_in((carry_decay, local_in[count]), "seq", chain_step, identity, False)[1]
    grad_in = carried_in((carry_decay, carried), "seq", chain_step, identity, True)[1]
    grad_feats = []
    grad_bcs = []
    for number in range(count):
        feat_blk, cot_blk, b_rows, c_rows, running = pieces[number]
        block_state = local_in[number] + jnp.exp(start_logs[number])[:, None, None] * state_in
        block_grad = local_out[number] + jnp.exp(after_logs[number])[:, None, None] * grad_in
        grad_feat, grad_bc = block_terms(
            halves_list[number],
            feat_blk,
            cot_blk,
            b_rows,
            c_rows,
            running,
            block_state,
            block_grad,
            skip_gain,
        )
        grad_feats.append(grad_feat)
        grad_bcs.append(grad_bc)
    grad_input = (
        jnp.concatenate(grad_feats, axis=0)
        .reshape(length, heads * head_dim)
        .astype(jnp.bfloat16)[None]
    )
    grad_bc_all = jnp.concatenate(grad_bcs, axis=0).astype(jnp.bfloat16)
    columns = layer_rows
    grad_sum = lax.psum_scatter(
        lax.dot_general(
            columns, grad_bc_all, (((0,), (0,)), ((), ())), preferred_element_type=jnp.float32
        ),
        ("seq", "opt"),
        scatter_dimension=0,
        tiled=True,
    )
    col_raw, old_total = lax.psum(
        (jnp.sum(grad_sum * grad_sum, axis=0), jnp.sum(row_stat)), ("seq", "opt")
    )
    raw_total = jnp.sum(col_raw)
    factor = jnp.minimum(1.0, clip_norm / jnp.sqrt(raw_total + norm_floor))
    scaled = grad_sum * factor
    squares = scaled * scaled
    col_next = beta_two * col_stat + (1.0 - beta_two) * (
        factor * factor * col_raw / D + tiny_square
    )
    row_next = beta_two * row_stat + (1.0 - beta_two) * (jnp.mean(squares, axis=1) + tiny_square)
    row_mean = (
        beta_two * old_total
        + (1.0 - beta_two) * (factor * factor * raw_total / (2 * state_dim) + D * tiny_square)
    ) / D
    moment = beta_one * m_code.astype(jnp.float32) * m_scale[None, :] + (1.0 - beta_one) * scaled
    second = row_next[:, None] * col_next[None, :] / row_mean
    update = moment / (jnp.sqrt(second) + adam_floor) + weight_decay * w_bc
    col_peak = lax.pmax(jnp.max(jnp.abs(moment), axis=0), ("seq", "opt"))
    scale_next = col_peak + peak_floor
    code_next = (moment / scale_next[None, :]).astype(jnp.bfloat16)
    return (grad_input, update, code_next, scale_next, row_next, col_next)


def solution(mesh):
    return jax.shard_map(
        per_device,
        mesh=mesh,
        in_specs=(
            P("opt", "seq", None),
            P("opt", "seq", None),
            P("opt", "seq", None),
            P("opt", None, "seq"),
            P(),
            P(("seq", "opt"), None),
            P(("seq", "opt"), None),
            P(),
            P(("seq", "opt")),
            P(),
        ),
        out_specs=(
            P("opt", "seq", None),
            P(("seq", "opt"), None),
            P(("seq", "opt"), None),
            P(),
            P(("seq", "opt")),
            P(),
        ),
        check_vma=False,
    )
```

profile of v0, /device:TPU:0, one launch (start us, length us, event | category | flops | bytes accessed | tf_op | source)
XLA Modules:
  0.0 816.2 jit_solution(16822192327732359198)
XLA Ops:
  11.2 6.4 copy.108
  18.2 3.8 fusion.87
  22.0 48.3 %all-gather.7.cloned.1.call-done = bf16[4096,256]{1,0:T(8,128)(2,1)} async-done(((bf16[128,256]{1,0:T(8,128)(2,1)}), bf16[4096,256]{1,0:T(8,128)(2,1)}) %all-gather.7.cloned.1.call-update) | async-done | bytes 2097168 | tf_op jit(solution)/shard_map/all_gather | solution.py:102
  70.4 4.1 fusion.50
  74.8 3.9 fusion.26
  80.0 3.6 multiply_add_fusion.2
  83.9 4.7 fusion.85
  88.6 3.5 copy.155
  92.1 4.8 copy.156
  100.7 3.6 multiply_add_fusion
  106.5 21.2 %all-reduce = f32[256]{0:T(256)S(1)} all-reduce(f32[256]{0:T(256)S(1)} %dynamic-update-slice), channel_id=2, replica_groups=mesh['seq'=8,'opt'=4] {'seq'}, use_global_device_ids=true, to_apply=%add | all-reduce | flops 256 | bytes 2048
  127.8 4.1 multiply_reduce_fusion.1
  131.9 3.0 multiply_reduce_fusion
  135.0 175.3 %all-gather.9.cloned.1.call-done = f32[256,128,128]{2,1,0:T(8,128)} async-done(((f32[32,128,128]{2,1,0:T(8,128)}), f32[256,128,128]{2,1,0:T(8,128)}) %all-gather.9.cloned.1.call-update) | async-done | bytes 16777232 | tf_op jit(solution)/shard_map/all_gather | solution.py:25
  310.5 15.5 %while.26 = (s32[]{:T(128)}, f32[32,128,128]{2,1,0:T(8,128)S(1)}, s32[]{:T(128)}, f32[8,32]{1,0:T(8,128)S(1)}, f32[8,32,128,128]{3,2,1,0:T(8,128)}, /*index=5*/s32[]{:T(128)}, s32[]{:T(128)}, s32[]{:T(128)}, s32[]{:T(128)}) while((s32[]{:T(128)}, f32[32,128,128]{2,1,0:T(8,128)S(1)}, s32[]{:T(128)}, f32[8,32]{1,0:T(8,128)S(1)}, ...), condition=%wide.region_5.6_spmd, body=%wide.region_4.5_spmd.sunk | while | flops 1048582 | bytes 6291995 | solution.py:34
  321.3 2.4 bitcast_add_fusion.6
  326.0 3.7 multiply_reduce_fusion.3
  331.9 206.0 %all-gather.11.cloned.1.call-done = f32[256,128,128]{2,1,0:T(8,128)} async-done(((f32[32,128,128]{2,1,0:T(8,128)}), f32[256,128,128]{2,1,0:T(8,128)}) %all-gather.11.cloned.1.call-update) | async-done | bytes 16777232 | tf_op jit(solution)/shard_map/all_gather | solution.py:25
  539.5 5.1 multiply_reduce_fusion.2
  547.8 3.2 convolution_bitcast_fusion
  552.1 6.1 fusion.86
  558.2 5.8 copy.118
  564.1 5.6 copy.120
  570.7 7.3 fusion
  578.0 5.5 fusion.5
  583.6 3.4 fusion.11
  587.0 4.0 fusion.13
  593.3 6.6 copy.121
  599.8 119.3 %reduce-scatter.2.cloned.1.call-done = f32[128,256]{0,1:T(8,128)} async-done(((f32[4096,256]{0,1:T(8,128)}), f32[128,256]{0,1:T(8,128)}) %reduce-scatter.2.cloned.1.call-update) | async-done | bytes 131088 | tf_op jit(solution)/shard_map/reduce_scatter | solution.py:188
  720.1 6.4 copy.138
  726.5 37.0 %all-reduce.1 = (f32[]{:T(128)}, f32[256]{0:T(256)S(1)}) all-reduce(f32[]{:T(128)} %reduce_sum.111, f32[256]{0:T(256)S(1)} %multiply_reduce_fusion.7), channel_id=1, replica_groups=mesh['seq'=8,'opt'=4] {'seq','opt'}, use_global_device_ids=true, to_apply=%region_20.21 | all-reduce | flops 257 | bytes 2056 | tf_op jit(solution)/shard_map/psum | solution.py:196
  765.7 41.2 %pmax.7 = f32[256]{0:T(256)S(1)} all-reduce(f32[256]{0:T(256)S(1)} %get-tuple-element.160), channel_id=1, replica_groups=mesh['seq'=8,'opt'=4] {'seq','opt'}, use_global_device_ids=true, to_apply=%region_22.23 | all-reduce | flops 256 | bytes 2048 | tf_op jit(solution)/shard_map/pmax | solution.py:214
  (131 shorter events, 39.3 us)
Async XLA Ops:
  7.2 63.2 %all-gather.7.cloned.1.call-start = ((), (), s32[]{:S(2)}) async-start(), calls=%async_computation.1 | async-start | bytes 2162688 | tf_op jit(solution)/shard_map/all_gather | solution.py:102
  8.8 301.5 %all-gather.9.cloned.1.call-start = ((), (), s32[]{:S(2)}) async-start(), calls=%async_computation.3 | async-start | bytes 18874368 | tf_op jit(solution)/shard_map/all_gather | solution.py:25
  22.0 56.7 %copy-start.9 = (bf16[1,256,4096]{1,2,0:T(8,128)(2,1)}, bf16[1,256,4096]{1,2,0:T(8,128)(2,1)S(1)}, u32[]{:S(2)}) copy-start(bf16[1,256,4096]{1,2,0:T(8,128)(2,1)S(1)} %get-tuple-element.191) | copy-start | bytes 6291460
  78.7 1.3 copy-start.1
  83.6 454.3 %all-gather.11.cloned.1.call-start = ((), (), s32[]{:S(2)}) async-start(), calls=%async_computation.4 | async-start | bytes 18874368 | tf_op jit(solution)/shard_map/all_gather | solution.py:25
  92.1 35.7 %copy-start.5 = (bf16[1,256,4096]{1,2,0:T(8,128)(2,1)}, bf16[1,256,4096]{1,2,0:T(8,128)(2,1)S(1)}, u32[]{:S(2)}) copy-start(bf16[1,256,4096]{1,2,0:T(8,128)(2,1)S(1)} %copy.155) | copy-start | bytes 6291460
  97.1 3.6 copy-start.7
  99.4 1.3 copy-start.4
  104.3 0.7 copy-start.26
  104.4 614.7 %reduce-scatter.2.cloned.1.call-start = ((), (), s32[]{:S(2)}) async-start(), calls=%async_computation.2 | async-start | bytes 4325376 | tf_op jit(solution)/shard_map/reduce_scatter | solution.py:188
  127.8 4.1 copy-start.8
  127.8 4.1 copy-start.12
  326.0 3.8 copy-start.2
  326.0 3.8 copy-start.6
  539.5 5.1 copy-start
  539.5 5.1 copy-start.10
  544.6 3.2 copy-start.15
  551.0 0.9 copy-start.17
  551.0 1.0 copy-start.18
  564.0 5.6 copy-start.25
  564.0 6.2 copy-start.23
  570.7 7.3 copy-start.11
  578.0 5.6 copy-start.14
  578.0 5.6 copy-start.21
  583.5 3.4 copy-start.3
  583.5 3.4 copy-start.13
  720.1 45.4 %copy-start.22 = (f32[256]{0:T(256)S(1)}, f32[256]{0:T(256)}, u32[]{:S(2)}) copy-start(f32[256]{0:T(256)} %param.23) | copy-start | bytes 3076
  720.1 45.4 %copy-start.16 = (f32[128,256]{0,1:T(8,128)S(1)}, f32[128,256]{0,1:T(8,128)}, u32[]{:S(2)}) copy-start(f32[128,256]{0,1:T(8,128)} %reduce-scatter.2.cloned.1.call-done) | copy-start | bytes 393220
  765.5 43.7 %copy-start.19 = (f32[256]{0:T(256)}, f32[256]{0:T(256)S(1)}, u32[]{:S(2)}) copy-start(f32[256]{0:T(256)S(1)} %multiply_add_fusion.5) | copy-start | bytes 3076
  806.9 2.4 copy-start.20
  806.9 2.4 copy-start.24
Sparse Core Ops, SparseCore 0:
  11.4 58.9 all-gather.6
  83.8 226.4 all-gather.8
  312.4 225.4 all-gather.10
  551.2 167.8 reduce-scatter.1
where the time goes:
time: 823 us; the launch traced here: 816 us
  waiting for transfers between devices  549 us (67%)
  blocking collectives  99.4 us (12%)
  local copies, waits for them, and re-layouts  63.8 us (8%)
  matrix products  62.4 us (8%)
  other arithmetic  23.3 us (3%)
  between operations  17.5 us (2%)
    all_gather x2, waiting for transfers between devices, carried_in(): gathered = jax.tree.map(lambda a: lax.all_gather(a, axis), part)  381 us
    reduce_scatter x1, waiting for transfers between devices, per_device(): lax.psum_scatter(lax.dot_general(columns, grad_bc_all, (((0,), (0,)), (()...  119 us
    all_gather x1, waiting for transfers between devices, per_device(): lax.all_gather(w_half, ('seq', 'opt'), axis=0, tiled=True)  48.3 us
    pmax x1, blocking collectives, per_device(): col_peak = lax.pmax(jnp.max(jnp.abs(moment), axis=0), ('seq', 'opt'))  41.2 us
    psum x1, blocking collectives, per_device(): lax.psum((jnp.sum(grad_sum * grad_sum, axis=0), jnp.sum(row_stat)), ('seq...  37 us
    unnamed x66, local copies, waits for them, and re-layouts  28.5 us
    slice x4, local copies, waits for them, and re-layouts, per_device(): cots[lower_end:upper_end]  21.3 us
    unnamed x1, blocking collectives  21.2 us
  transfers between devices with their start and end apart: 4, of which 4 were waited for; matrix products, arithmetic and copies ran while one was open for 13% of the time, Pallas kernels for 0%

commit v1 on v0

v1 whole, which is shorter than its diff:
```python
import functools

import jax
import jax.numpy as jnp
from jax import lax
from jax.experimental import pallas as pl
from jax.experimental.pallas import tpu as pltpu
from jax.sharding import PartitionSpec as P

BLOCK = 256
LANES = 128

beta_one = 0.9
beta_two = 0.95
weight_decay = 0.1
clip_norm = 1.0
tiny_square = 1e-30
adam_floor = 1e-08
peak_floor = 1e-06
norm_floor = 1e-06
highest = lax.Precision.HIGHEST
MESH = pl.DeviceIdType.MESH
VMEM_LIMIT = 60 * 1024 * 1024
f32 = jnp.float32
bf16 = jnp.bfloat16


def dot_nn(a, b):
    return lax.dot_general(a, b, (((1,), (0,)), ((), ())), preferred_element_type=f32)


def dot_nt(a, b):
    return lax.dot_general(a, b, (((1,), (1,)), ((), ())), preferred_element_type=f32)


def dot_tn(a, b):
    return lax.dot_general(a, b, (((0,), (0,)), ((), ())), preferred_element_type=f32)


def as_column(row):
    return jnp.transpose(jnp.broadcast_to(row, (LANES, row.shape[1])))


def widened(column, length):
    return jnp.concatenate([column] * (length // LANES), axis=1)


def mixing_kernel(count, x_ref, dy_ref, run_ref, mix_ref):
    @pl.when(pl.program_id(0) == 0)
    def _():
        mix_ref[...] = jnp.zeros_like(mix_ref)

    row_pos = lax.broadcasted_iota(jnp.int32, (BLOCK, BLOCK), 0)
    col_pos = lax.broadcasted_iota(jnp.int32, (BLOCK, BLOCK), 1)
    for b in range(count):
        rows = slice(b * BLOCK, (b + 1) * BLOCK)
        row = run_ref[0, b : b + 1, :]
        spread = widened(as_column(row), BLOCK) - row
        decays = jnp.exp(jnp.where(row_pos >= col_pos, spread, -jnp.inf))
        mix_ref[b] += decays * dot_nt(dy_ref[rows, :], x_ref[rows, :])


def local_kernel(count, x_ref, dy_ref, b_ref, c_ref, run_ref, send_ref, starts_ref, outs_ref):
    adds = []
    for b in range(count):
        rows = slice(b * BLOCK, (b + 1) * BLOCK)
        row = run_ref[0, b : b + 1, :]
        column = as_column(row)
        closing = row[:, BLOCK - 1 : BLOCK]
        b_scaled = (b_ref[rows, :].astype(f32) * jnp.exp(closing - column)).astype(bf16)
        c_scaled = (c_ref[rows, :].astype(f32) * jnp.exp(column)).astype(bf16)
        adds.append(
            (jnp.exp(closing), dot_tn(b_scaled, x_ref[rows, :]), dot_tn(c_scaled, dy_ref[rows, :]))
        )
    state = None
    for b in range(count):
        starts_ref[0, b] = (jnp.zeros_like(adds[b][1]) if state is None else state).astype(bf16)
        state = adds[b][1] if state is None else adds[b][0] * state + adds[b][1]
    send_ref[0, 0, 0] = state.astype(bf16)
    carried = None
    for b in reversed(range(count)):
        outs_ref[0, b] = (jnp.zeros_like(adds[b][2]) if carried is None else carried).astype(bf16)
        carried = adds[b][2] if carried is None else adds[b][0] * carried + adds[b][2]
    send_ref[0, 1, 0] = carried.astype(bf16)


def grads_kernel(
    count, skip_ref, x_ref, dy_ref, b_ref, c_ref, run_ref, starts_ref, outs_ref, far_ref, mix_ref,
    gx_ref, gbc_ref, affinity, acc_b, acc_c,
):
    h = pl.program_id(0)
    state_dim = b_ref.shape[1]

    @pl.when(h == 0)
    def _():
        acc_b[...] = jnp.zeros_like(acc_b)
        acc_c[...] = jnp.zeros_like(acc_c)
        for b in range(count):
            rows = slice(b * BLOCK, (b + 1) * BLOCK)
            affinity[b] = dot_nt(b_ref[rows, :], c_ref[rows, :])

    row_pos = lax.broadcasted_iota(jnp.int32, (BLOCK, BLOCK), 0)
    col_pos = lax.broadcasted_iota(jnp.int32, (BLOCK, BLOCK), 1)
    closings = [run_ref[0, b : b + 1, BLOCK - 1 : BLOCK] for b in range(count)]
    for b in range(count):
        rows = slice(b * BLOCK, (b + 1) * BLOCK)
        row = run_ref[0, b : b + 1, :]
        column = as_column(row)
        before = sum(closings[:b], jnp.zeros((1, 1), f32))
        after = sum(closings[b + 1 :], jnp.zeros((1, 1), f32))
        far_state = far_ref[0, 0, 0].astype(f32)
        far_grad = far_ref[0, 1, 0].astype(f32)
        state_in = (starts_ref[0, b].astype(f32) + jnp.exp(before) * far_state).astype(bf16)
        grad_in = (outs_ref[0, b].astype(f32) + jnp.exp(after) * far_grad).astype(bf16)
        grow = jnp.exp(column)
        shrink = jnp.exp(closings[b] - column)
        x_blk = x_ref[rows, :]
        dy_blk = dy_ref[rows, :]
        spread = row - widened(column, BLOCK)
        decays = jnp.exp(jnp.where(col_pos >= row_pos, spread, -jnp.inf))
        weighted = (decays * affinity[b]).astype(bf16)
        inner = dot_nn(weighted, dy_blk)
        outer = dot_nn(b_ref[rows, :], grad_in) * shrink
        gx_ref[rows, :] = (inner + outer + skip_ref[h] * dy_blk.astype(f32)).astype(bf16)
        acc_c[rows, :] += grow * dot_nt(dy_blk, state_in)
        acc_b[rows, :] += shrink * dot_nt(x_blk, grad_in)

    @pl.when(h == pl.num_programs(0) - 1)
    def _():
        for b in range(count):
            rows = slice(b * BLOCK, (b + 1) * BLOCK)
            mixing = mix_ref[b].astype(bf16)
            gbc_ref[rows, :state_dim] = (acc_b[rows, :] + dot_tn(mixing, c_ref[rows, :])).astype(bf16)
            gbc_ref[rows, state_dim:] = (acc_c[rows, :] + dot_nn(mixing, b_ref[rows, :])).astype(bf16)


def swap_all(n, me, src_of, dst_of, device_of, send_sem, recv_sem):
    def copy_to(distance):
        other = lax.rem(me + distance, n)
        return pltpu.make_async_remote_copy(
            src_ref=src_of(other), dst_ref=dst_of(me), send_sem=send_sem.at[other],
            recv_sem=recv_sem.at[me], device_id=device_of(other), device_id_type=MESH,
        )

    def copy_from(distance):
        other = lax.rem(me + distance, n)
        return pltpu.make_async_remote_copy(
            src_ref=src_of(other), dst_ref=dst_of(other), send_sem=send_sem.at[other],
            recv_sem=recv_sem.at[other], device_id=device_of(other), device_id_type=MESH,
        )

    def start(distance, carry):
        copy_to(distance).start()
        return carry

    def finish(distance, carry):
        copy = copy_from(distance)
        copy.wait_send()
        copy.wait_recv()
        return carry

    lax.fori_loop(1, n, start, 0)
    return lambda: lax.fori_loop(1, n, finish, 0)


def greet(n, me, device_of):
    barrier = pltpu.get_barrier_semaphore()

    def signal(distance, carry):
        other = lax.rem(me + distance, n)
        pl.semaphore_signal(barrier, inc=1, device_id=device_of(other), device_id_type=MESH)
        return carry

    lax.fori_loop(1, n, signal, 0)
    pl.semaphore_wait(barrier, n - 1)


def carry_kernel(
    n, send_ref, decay_ref, out_ref, got, got_decay, prefix, landed, run,
    send_a, recv_a, send_d, recv_d, send_b, recv_b,
):
    me = lax.axis_index("seq")
    opt = lax.axis_index("opt")

    def device_of(s):
        return (s, opt)

    greet(n, me, device_of)
    end_d = swap_all(
        n, me, lambda s: decay_ref.at[s], lambda s: got_decay.at[s], device_of, send_d, recv_d
    )
    end_a = swap_all(n, me, lambda s: send_ref.at[s], lambda s: got.at[s], device_of, send_a, recv_a)
    end_d()
    end_a()
    got[me] = send_ref[me]
    got_decay[me] = decay_ref[me]

    run[...] = jnp.zeros_like(run)

    def forward(s, carry):
        state = run[0]
        prefix[s, 0] = state.astype(bf16)
        run[0] = got_decay[s] * state + got[s, 0].astype(f32)
        return carry

    def backward(lap, carry):
        s = n - 1 - lap
        state = run[1]
        prefix[s, 1] = state.astype(bf16)
        run[1] = got_decay[s] * state + got[s, 1].astype(f32)
        return carry

    lax.fori_loop(0, n, forward, 0)
    lax.fori_loop(0, n, backward, 0)
    swap_all(n, me, lambda s: prefix.at[s], lambda s: landed.at[s], device_of, send_b, recv_b)()
    landed[me] = prefix[me]
    out_ref[...] = landed[...]


def step_kernel(
    n_seq, n_opt, part_ref, w_ref, code_ref, scale_ref, row_ref, col_ref,
    update_ref, code_out, scale_out, row_out, col_out,
    got_a, mid, got_b, stats, all_stats, peak, all_peaks,
    send_a, recv_a, send_b, recv_b, send_c, recv_c, send_d, recv_d,
):
    seq = lax.axis_index("seq")
    opt = lax.axis_index("opt")
    n = n_seq * n_opt
    me = seq * n_opt + opt

    def any_device(i):
        return (i // n_opt, lax.rem(i, n_opt))

    greet(n, me, any_device)
    swap_all(
        n_opt, opt, lambda o: part_ref.at[o], lambda o: got_a.at[o],
        lambda o: (seq, o), send_a, recv_a,
    )()
    got_a[opt] = part_ref[opt]

    def fold(s, carry):
        total = got_a[0, s].astype(f32)
        for o in range(1, n_opt):
            total += got_a[o, s].astype(f32)
        mid[s] = total.astype(bf16)
        return carry

    lax.fori_loop(0, n_seq, fold, 0)
    swap_all(
        n_seq, seq, lambda s: mid.at[s], lambda s: got_b.at[s],
        lambda s: (s, opt), send_b, recv_b,
    )()
    got_b[seq] = mid[seq]
    grad = got_b[0].astype(f32)
    for s in range(1, n_seq):
        grad += got_b[s].astype(f32)

    rows, cols = grad.shape
    width = n * rows
    squares_raw = grad * grad
    stats[:, :cols] = jnp.sum(squares_raw, axis=0, keepdims=True)
    row_stat = row_ref[...]
    stats[:, cols:] = jnp.broadcast_to(jnp.sum(row_stat, axis=0, keepdims=True), (1, LANES))
    swap_all(
        n, me, lambda i: stats, lambda i: all_stats.at[i], any_device, send_c, recv_c
    )()
    all_stats[me] = stats[...]
    sums = all_stats[0]
    for i in range(1, n):
        sums += all_stats[i]
    col_raw = sums[:, :cols]
    old_total = sums[:, cols : cols + 1]
    raw_total = jnp.sum(col_raw, axis=1, keepdims=True)
    factor = jnp.minimum(1.0, clip_norm / jnp.sqrt(raw_total + norm_floor))
    scaled = grad * factor
    moment = beta_one * code_ref[...].astype(f32) * scale_ref[...] + (1.0 - beta_one) * scaled
    peak[...] = jnp.max(jnp.abs(moment), axis=0, keepdims=True)
    end_peaks = swap_all(
        n, me, lambda i: peak, lambda i: all_peaks.at[i], any_device, send_d, recv_d
    )
    col_next = beta_two * col_ref[...] + (1.0 - beta_two) * (
        factor * factor * col_raw / width + tiny_square
    )
    row_next = beta_two * row_stat + (1.0 - beta_two) * (
        jnp.sum(scaled * scaled, axis=1, keepdims=True) / cols + tiny_square
    )
    row_mean = (
        beta_two * old_total
        + (1.0 - beta_two) * (factor * factor * raw_total / cols + width * tiny_square)
    ) / width
    second = row_next * col_next / row_mean
    update_ref[...] = moment / (jnp.sqrt(second) + adam_floor) + weight_decay * w_ref[...]
    row_out[...] = row_next
    col_out[...] = col_next
    end_peaks()
    all_peaks[me] = peak[...]
    scale_next = all_peaks[0]
    for i in range(1, n):
        scale_next = jnp.maximum(scale_next, all_peaks[i])
    scale_next = scale_next + peak_floor
    scale_out[...] = scale_next
    code_out[...] = (moment / scale_next).astype(bf16)


def params(**more):
    return pltpu.CompilerParams(vmem_limit_bytes=VMEM_LIMIT, **more)


def whole():
    return pl.BlockSpec(memory_space=pltpu.VMEM)


def dma(*counts):
    return [pltpu.SemaphoreType.DMA((count,)) for count in counts for _ in range(2)]


def per_device(
    n_seq, n_opt, layer_in, ssm_input, grad_out, log_decay, skip_gain, w_bc, m_code, m_scale,
    row_stat, col_stat,
):
    layer_rows = layer_in[0]
    x = ssm_input[0]
    dy = grad_out[0]
    length, width = layer_rows.shape
    heads = skip_gain.shape[0]
    head_dim = x.shape[1] // heads
    state_dim = w_bc.shape[1] // 2
    count = length // BLOCK
    group = heads // n_seq
    own_rows = w_bc.shape[0]

    w_all = lax.all_gather(w_bc.astype(bf16), ("seq", "opt"), axis=0, tiled=True)

    ones = (
        lax.broadcasted_iota(jnp.int32, (BLOCK, BLOCK), 0)
        <= lax.broadcasted_iota(jnp.int32, (BLOCK, BLOCK), 1)
    ).astype(f32)
    running = jnp.dot(
        log_decay[0].reshape(heads * count, BLOCK), ones, precision=highest
    ).reshape(heads, count, BLOCK)
    decay = jnp.exp(jnp.sum(running[:, :, BLOCK - 1], axis=1))
    decay = jnp.broadcast_to(decay[:, None], (heads, LANES)).reshape(n_seq, group, 1, LANES)

    tokens = pl.BlockSpec((length, head_dim), lambda h: (0, h))
    run_spec = pl.BlockSpec((1, count, BLOCK), lambda h: (h, 0, 0))
    mix_spec = pl.BlockSpec((count, BLOCK, BLOCK), lambda h: (0, 0, 0))
    state_spec = pl.BlockSpec((1, count, state_dim, head_dim), lambda h: (h, 0, 0, 0))
    far_spec = pl.BlockSpec(
        (1, 2, 1, state_dim, head_dim), lambda h: (h // group, 0, h % group, 0, 0)
    )
    b_spec = pl.BlockSpec((length, state_dim), lambda h: (0, 0))
    c_spec = pl.BlockSpec((length, state_dim), lambda h: (0, 1))
    far_shape = (n_seq, 2, group, state_dim, head_dim)
    square = heads * length * BLOCK

    mixing = pl.pallas_call(
        functools.partial(mixing_kernel, count),
        grid=(heads,),
        in_specs=[tokens, tokens, run_spec],
        out_specs=mix_spec,
        out_shape=jax.ShapeDtypeStruct((count, BLOCK, BLOCK), f32),
        compiler_params=params(),
        cost_estimate=pl.CostEstimate(
            flops=2 * square * head_dim * 10, bytes_accessed=4 * length * width, transcendentals=square
        ),
        name="mixing",
    )(x, dy, running)

    proj = jnp.dot(layer_rows, w_all, preferred_element_type=f32).astype(bf16)

    sent, starts, outs = pl.pallas_call(
        functools.partial(local_kernel, count),
        grid=(heads,),
        in_specs=[tokens, tokens, b_spec, c_spec, run_spec],
        out_specs=[far_spec, state_spec, state_spec],
        out_shape=[
            jax.ShapeDtypeStruct(far_shape, bf16),
            jax.ShapeDtypeStruct((heads, count, state_dim, head_dim), bf16),
            jax.ShapeDtypeStruct((heads, count, state_dim, head_dim), bf16),
        ],
        compiler_params=params(),
        name="local_states",
    )(x, dy, proj, proj, running)

    far = pl.pallas_call(
        functools.partial(carry_kernel, n_seq),
        in_specs=[whole(), whole()],
        out_specs=whole(),
        out_shape=jax.ShapeDtypeStruct(far_shape, bf16),
        scratch_shapes=[
            pltpu.VMEM(far_shape, bf16),
            pltpu.VMEM((n_seq, group, 1, LANES), f32),
            pltpu.VMEM(far_shape, bf16),
            pltpu.VMEM(far_shape, bf16),
            pltpu.VMEM(far_shape[1:], f32),
        ]
        + dma(n_seq, n_seq, n_seq),
        compiler_params=params(collective_id=0, has_side_effects=True),
        name="carry_states",
    )(sent, decay)

    grad_input, grad_bc = pl.pallas_call(
        functools.partial(grads_kernel, count),
        grid=(heads,),
        in_specs=[
            pl.BlockSpec(memory_space=pltpu.SMEM), tokens, tokens, b_spec, c_spec, run_spec,
            state_spec, state_spec, far_spec, mix_spec,
        ],
        out_specs=[tokens, pl.BlockSpec((length, 2 * state_dim), lambda h: (0, 0))],
        out_shape=[
            jax.ShapeDtypeStruct(x.shape, bf16),
            jax.ShapeDtypeStruct((length, 2 * state_dim), bf16),
        ],
        scratch_shapes=[
            pltpu.VMEM((count, BLOCK, BLOCK), f32),
            pltpu.VMEM((length, state_dim), f32),
            pltpu.VMEM((length, state_dim), f32),
        ],
        compiler_params=params(),
        name="grads",
    )(skip_gain, x, dy, proj, proj, running, starts, outs, far, mixing)

    cols = 2 * state_dim
    part = lax.dot_general(
        layer_rows, grad_bc, (((0,), (0,)), ((), ())), preferred_element_type=f32
    ).astype(bf16)
    part = jnp.transpose(part.reshape(n_seq, n_opt, own_rows, cols), (1, 0, 2, 3))

    n = n_seq * n_opt
    update, code_next, scale_next, row_next, col_next = pl.pallas_call(
        functools.partial(step_kernel, n_seq, n_opt),
        in_specs=[whole()] * 6,
        out_specs=[whole()] * 5,
        out_shape=[
            jax.ShapeDtypeStruct((own_rows, cols), f32),
            jax.ShapeDtypeStruct((own_rows, cols), bf16),
            jax.ShapeDtypeStruct((1, cols), f32),
            jax.ShapeDtypeStruct((own_rows, 1), f32),
            jax.ShapeDtypeStruct((1, cols), f32),
        ],
        scratch_shapes=[
            pltpu.VMEM((n_opt, n_seq, own_rows, cols), bf16),
            pltpu.VMEM((n_seq, own_rows, cols), bf16),
            pltpu.VMEM((n_seq, own_rows, cols), bf16),
            pltpu.VMEM((1, cols + LANES), f32),
            pltpu.VMEM((n, 1, cols + LANES), f32),
            pltpu.VMEM((1, cols), f32),
            pltpu.VMEM((n, 1, cols), f32),
        ]
        + dma(n_opt, n_seq, n, n),
        compiler_params=params(collective_id=1, has_side_effects=True),
        name="sum_and_step",
    )(part, w_bc, m_code, m_scale[None, :], row_stat[:, None], col_stat[None, :])
    return (grad_input[None], update, code_next, scale_next[0], row_next[:, 0], col_next[0])


def solution(mesh):
    return jax.shard_map(
        functools.partial(per_device, mesh.shape["seq"], mesh.shape["opt"]),
        mesh=mesh,
        in_specs=(
            P("opt", "seq", None),
            P("opt", "seq", None),
            P("opt", "seq", None),
            P("opt", None, "seq"),
            P(),
            P(("seq", "opt"), None),
            P(("seq", "opt"), None),
            P(),
            P(("seq", "opt")),
            P(),
        ),
        out_specs=(
            P("opt", "seq", None),
            P(("seq", "opt"), None),
            P(("seq", "opt"), None),
            P(),
            P(("seq", "opt")),
            P(),
        ),
        check_vma=False,
    )
```

time: 823 us -> 313 us (0.38)
  waiting for transfers between devices: 549 us -> 37.4 us
  Pallas kernels: 0 us -> 233 us
  blocking collectives: 99.4 us -> 0 us
  matrix products: 62.4 us -> 8.6 us
  local copies, waits for them, and re-layouts: 63.8 us -> 14.2 us
  other arithmetic: 23.3 us -> 3.49 us
    all_gather x3 -> x1, waiting for transfers between devices: 430 us -> 37.3 us  [per_device(): lax.all_gather(w_bc.astype(bf16), ('seq', 'opt'), axis=0, tiled=True)]
    pallas_call x0 -> x5, Pallas kernels: none -> 233 us  [the longest x1 93.2 us: per_device(): pl.pallas_call(functools.partial(carry_kernel, n_seq), in_specs=[whole(),...]
    reduce_scatter x1 -> x0, waiting for transfers between devices: 119 us -> none  [per_device(): lax.psum_scatter(lax.dot_general(columns, grad_bc_all, (((0,), (0,)), (()...]
    dot_general x22 -> x3, matrix products: 62.4 us -> 8.6 us  [the longest x1 4.84 us: per_device(): proj = jnp.dot(layer_rows, w_all, preferred_element_type=f32).astype(bf16)]
    pmax x1 -> x0, blocking collectives: 41.2 us -> none  [per_device(): col_peak = lax.pmax(jnp.max(jnp.abs(moment), axis=0), ('seq', 'opt'))]
    psum x1 -> x0, blocking collectives: 37 us -> none  [per_device(): lax.psum((jnp.sum(grad_sum * grad_sum, axis=0), jnp.sum(row_stat)), ('seq...]
    slice x11 -> x0, local copies, waits for them, and re-layouts: 26.6 us -> none  [the longest x4 21.3 us: per_device(): cots[lower_end:upper_end]]
    unnamed x66 -> x6, local copies, waits for them, and re-layouts: 28.5 us -> 5.5 us
  transfers between devices with their start and end apart: 4 -> 1, of which waited for: 4 -> 1; matrix products, arithmetic and copies ran while one was open for 13% -> 1% of each run, Pallas kernels for 0% -> 7%
where the time goes in v1:
time: 313 us; the launch traced here: 311 us
  Pallas kernels  233 us (74%)
  waiting for transfers between devices  37.4 us (12%)
  local copies, waits for them, and re-layouts  14.2 us (5%)
  between operations  14.1 us (5%)
  matrix products  8.6 us (3%)
  other arithmetic  3.49 us (1%)
    pallas_call x1, Pallas kernels, per_device(): pl.pallas_call(functools.partial(carry_kernel, n_seq), in_specs=[whole(),...  93.2 us
    pallas_call x1, Pallas kernels, per_device(): pl.pallas_call(functools.partial(step_kernel, n_seq, n_opt), in_specs=[wh...  66.1 us
    all_gather x1, waiting for transfers between devices, per_device(): lax.all_gather(w_bc.astype(bf16), ('seq', 'opt'), axis=0, tiled=True)  37.3 us
    pallas_call x1, Pallas kernels, per_device(): pl.pallas_call(functools.partial(grads_kernel, count), grid=(heads,), in_...  27.8 us
    pallas_call x1, Pallas kernels, per_device(): pl.pallas_call(functools.partial(local_kernel, count), grid=(heads,), in_...  25.1 us
    pallas_call x1, Pallas kernels, per_device(): pl.pallas_call(functools.partial(mixing_kernel, count), grid=(heads,), in...  21.1 us
  transfers between devices with their start and end apart: 1, of which 1 were waited for; matrix products, arithmetic and copies ran while one was open for 1% of the time, Pallas kernels for 7%

profile of v1, /device:TPU:0, one launch (start us, length us, event | category | flops | bytes accessed | tf_op | source)
XLA Modules:
  0.0 311.0 jit_solution(2071508814863442188)
XLA Ops:
  7.2 0.0 all-gather.2.cloned.1.call-start
  7.2 1.5 convert_element_type.13
  8.8 0.0 all-gather.2.cloned.1.call-update
  8.8 0.9 reshape_squeeze.3
  9.6 0.2 convolution_bitcast_fusion
  9.9 0.0 copy-start
  9.9 0.5 slice_reduce_fusion
  10.4 0.1 exp.11
  10.5 1.4 copy.19.row_ref
  11.9 0.0 copy-done
  11.9 21.1 %mixing.1.mix_ref = f32[2,256,256]{2,1,0:T(8,128)} custom-call(bf16[512,4096]{1,0:T(8,128)(2,1)} %bitcast.26, bf16[512,4096]{1,0:T(8,128)(2,1)} %bitcast.29, f32[32,2,256]{2,1,0:T(2,128)} %copy-done), custom_call_target="tpu_custom_call" | custom-call | flops 10737418240 | bytes 8388608 | tf_op jit(solution)/shard_map/mixing/pallas_call | solution.py:356
  33.0 37.3 %all-gather.2.cloned.1.call-done = bf16[4096,256]{1,0:T(8,128)(2,1)} async-done(((bf16[128,256]{1,0:T(8,128)(2,1)}), bf16[4096,256]{1,0:T(8,128)(2,1)}) %all-gather.2.cloned.1.call-update) | async-done | bytes 2097168 | tf_op jit(solution)/shard_map/all_gather | solution.py:332
  70.4 4.8 %fusion.4.b_ref.c_ref = bf16[512,256]{1,0:T(8,128)(2,1)} fusion(bf16[4096,256]{1,0:T(8,128)(2,1)} %all-gather.2.cloned.1.call-done, bf16[1,512,4096]{2,1,0:T(8,128)(2,1)} %param.10), kind=kOutput, calls=%fused_computation.6 | convolution fusion | flops 1073872896 | bytes 6553600 | tf_op jit(solution)/shard_map/dot_general | solution.py:369
  75.2 25.1 %local_states.1 = (bf16[8,2,4,128,128]{4,3,2,1,0:T(8,128)(2,1)}, bf16[32,2,128,128]{3,2,1,0:T(8,128)(2,1)}, bf16[32,2,128,128]{3,2,1,0:T(8,128)(2,1)}) custom-call(bf16[512,4096]{1,0:T(8,128)(2,1)} %bitcast.27, bf16[512,4096]{1,0:T(8,128)(2,1)} %bitcast.30, bf16[512,256]{1,0:T(8,128)(2,1)} %fusion.4.b_ref.c_ref, bf16[512,256]{1,0:T(8,128)(2,1)} %fusion.4.b_ref.c_ref, ...), custom_call_target="tpu_custom_call" | custom-call | tf_op jit(solution)/shard_map/local_states/pallas_call | solution.py:371
  100.3 0.7 broadcast_in_dim.18.decay_ref
  101.0 93.2 %carry_states.1.far_ref = bf16[8,2,4,128,128]{4,3,2,1,0:T(8,128)(2,1)} custom-call(bf16[8,2,4,128,128]{4,3,2,1,0:T(8,128)(2,1)} %get-tuple-element.18.send_ref, f32[8,4,1,128]{3,2,1,0:T(1,128)} %broadcast_in_dim.18.decay_ref), custom_call_target="tpu_custom_call" | custom-call | tf_op jit(solution)/shard_map/carry_states/pallas_call | solution.py:385
  194.2 27.8 %grads.1 = (bf16[512,4096]{1,0:T(8,128)(2,1)}, bf16[512,256]{1,0:T(8,128)(2,1)}) custom-call(f32[32]{0:T(128)} %skip_ref.1, bf16[512,4096]{1,0:T(8,128)(2,1)} %bitcast.28, bf16[512,4096]{1,0:T(8,128)(2,1)} %bitcast.31, bf16[512,256]{1,0:T(8,128)(2,1)} %fusion.4.b_ref.c_ref, bf16[512,256]{1,0:T(8,128)(2,1)} %fusion.4.b_ref.c_ref, f32[32,2,256]{2,1,0:T(2,128)} %copy-done, ...), custom_call_target="tpu_custom_call" | custom-call | tf_op jit(solution)/shard_map/grads/pallas_call | solution.py:402
  221.9 3.6 %fusion = bf16[4096,256]{0,1:T(8,128)(2,1)S(1)} fusion(bf16[512,256]{1,0:T(8,128)(2,1)} %get-tuple-element.20, bf16[1,512,4096]{2,1,0:T(8,128)(2,1)} %param.10), kind=kOutput, calls=%fused_computation.1 | convolution fusion | flops 1074790400 | bytes 6553600 | tf_op jit(solution)/shard_map/dot_general | solution.py:424
  225.5 2.5 copy.17
  228.0 3.2 %copy.21 = bf16[8,4,128,256]{3,2,0,1:T(8,128)(2,1)} copy(bf16[8,4,128,256]{3,2,1,0:T(8,128)(2,1)} %bitcast.33) | data formatting | bytes 4194304 | tf_op jit(solution)/shard_map/reshape | solution.py:427
  231.1 66.1 %sum_and_step.1 = (f32[128,256]{1,0:T(8,128)}, bf16[128,256]{1,0:T(8,128)(2,1)}, f32[1,256]{1,0:T(1,128)}, f32[128,1]{1,0:T(8,128)}, f32[1,256]{1,0:T(1,128)}) custom-call(bf16[4,8,128,256]{3,2,1,0:T(8,128)(2,1)} %bitcast.32, f32[128,256]{1,0:T(8,128)} %w_ref.1, bf16[128,256]{1,0:T(8,128)(2,1)} %code_ref.1, f32[1,256]{1,0:T(1,128)} %bitcast.34, ...), custom_call_target="tpu_custom_call" | custom-call | tf_op jit(solution)/shard_map/sum_and_step/pallas_call | solution.py:430
  297.2 1.5 reduce.1
  298.7 1.6 copy.26
  300.2 1.5 copy.27
  301.7 1.2 copy.28
  302.9 1.2 copy.29
  (2 shorter events, 0.0 us)
Async XLA Ops:
  7.2 63.2 %all-gather.2.cloned.1.call-start = ((), (), s32[]{:S(2)}) async-start(), calls=%async_computation | async-start | bytes 2162688 | tf_op jit(solution)/shard_map/all_gather | solution.py:332
  9.9 2.0 copy-start
Sparse Core Ops, SparseCore 0:
  11.4 58.9 all-gather.1

commit v2 on v1

--- a/solution.py
+++ b/solution.py
@@ -45,10 +45,38 @@
     return jnp.concatenate([column] * (length // LANES), axis=1)
 
 
-def mixing_kernel(count, x_ref, dy_ref, run_ref, mix_ref):
-    @pl.when(pl.program_id(0) == 0)
+def mixing_kernel(
+    count, n_seq, n_opt, w_ref, x_ref, dy_ref, run_ref, mix_ref, w_out,
+    got, send_a, recv_a, send_b, recv_b,
+):
+    seq = lax.axis_index("seq")
+    opt = lax.axis_index("opt")
+    h = pl.program_id(0)
+    last = pl.num_programs(0) - 1
+
+    def over_seq():
+        return swap_all(
+            n_seq, seq, lambda s: w_ref, lambda s: got.at[opt, s],
+            lambda s: (s, opt), send_a, recv_a,
+        )
+
+    def over_opt():
+        return swap_all(
+            n_opt, opt, lambda o: got.at[opt], lambda o: got.at[o],
+            lambda o: (seq, o), send_b, recv_b,
+        )
+
+    @pl.when(h == 0)
     def _():
+        greet(n_seq * n_opt, seq * n_opt + opt, lambda i: (i // n_opt, lax.rem(i, n_opt)))
+        over_seq()[0]()
+        got[opt, seq] = w_ref[...]
         mix_ref[...] = jnp.zeros_like(mix_ref)
+
+    @pl.when(h == last // 2)
+    def _():
+        over_seq()[1]()
+        over_opt()[0]()
 
     row_pos = lax.broadcasted_iota(jnp.int32, (BLOCK, BLOCK), 0)
     col_pos = lax.broadcasted_iota(jnp.int32, (BLOCK, BLOCK), 1)
@@ -59,18 +87,35 @@
         decays = jnp.exp(jnp.where(row_pos >= col_pos, spread, -jnp.inf))
         mix_ref[b] += decays * dot_nt(dy_ref[rows, :], x_ref[rows, :])
 
-
-def local_kernel(count, x_ref, dy_ref, b_ref, c_ref, run_ref, send_ref, starts_ref, outs_ref):
+    @pl.when(h == last)
+    def _():
+        over_opt()[1]()
+
+        def place(s, carry):
+            for o in range(n_opt):
+                w_out[s, o] = got[o, s]
+            return carry
+
+        lax.fori_loop(0, n_seq, place, 0)
+
+
+def local_kernel(
+    count, x_ref, dy_ref, b_ref, c_ref, run_ref, send_ref, starts_ref, outs_ref, b_turned, c_turned
+):
+    @pl.when(pl.program_id(0) == 0)
+    def _():
+        b_turned[...] = jnp.transpose(b_ref[...].astype(f32))
+        c_turned[...] = jnp.transpose(c_ref[...].astype(f32))
+
     adds = []
     for b in range(count):
         rows = slice(b * BLOCK, (b + 1) * BLOCK)
         row = run_ref[0, b : b + 1, :]
-        column = as_column(row)
         closing = row[:, BLOCK - 1 : BLOCK]
-        b_scaled = (b_ref[rows, :].astype(f32) * jnp.exp(closing - column)).astype(bf16)
-        c_scaled = (c_ref[rows, :].astype(f32) * jnp.exp(column)).astype(bf16)
+        b_scaled = (b_turned[:, rows] * jnp.exp(closing - row)).astype(bf16)
+        c_scaled = (c_turned[:, rows] * jnp.exp(row)).astype(bf16)
         adds.append(
-            (jnp.exp(closing), dot_tn(b_scaled, x_ref[rows, :]), dot_tn(c_scaled, dy_ref[rows, :]))
+            (jnp.exp(closing), dot_nn(b_scaled, x_ref[rows, :]), dot_nn(c_scaled, dy_ref[rows, :]))
         )
     state = None
     for b in range(count):
@@ -159,8 +204,13 @@
         copy.wait_recv()
         return carry
 
-    lax.fori_loop(1, n, start, 0)
-    return lambda: lax.fori_loop(1, n, finish, 0)
+    return lambda: lax.fori_loop(1, n, start, 0), lambda: lax.fori_loop(1, n, finish, 0)
+
+
+def begin_swap(*args):
+    start, finish = swap_all(*args)
+    start()
+    return finish
 
 
 def greet(n, me, device_of):
@@ -186,10 +236,10 @@
         return (s, opt)
 
     greet(n, me, device_of)
-    end_d = swap_all(
+    end_d = begin_swap(
         n, me, lambda s: decay_ref.at[s], lambda s: got_decay.at[s], device_of, send_d, recv_d
     )
-    end_a = swap_all(n, me, lambda s: send_ref.at[s], lambda s: got.at[s], device_of, send_a, recv_a)
+    end_a = begin_swap(n, me, lambda s: send_ref.at[s], lambda s: got.at[s], device_of, send_a, recv_a)
     end_d()
     end_a()
     got[me] = send_ref[me]
@@ -212,7 +262,7 @@
 
     lax.fori_loop(0, n, forward, 0)
     lax.fori_loop(0, n, backward, 0)
-    swap_all(n, me, lambda s: prefix.at[s], lambda s: landed.at[s], device_of, send_b, recv_b)()
+    begin_swap(n, me, lambda s: prefix.at[s], lambda s: landed.at[s], device_of, send_b, recv_b)()
     landed[me] = prefix[me]
     out_ref[...] = landed[...]
 
@@ -232,7 +282,7 @@
         return (i // n_opt, lax.rem(i, n_opt))
 
     greet(n, me, any_device)
-    swap_all(
+    begin_swap(
         n_opt, opt, lambda o: part_ref.at[o], lambda o: got_a.at[o],
         lambda o: (seq, o), send_a, recv_a,
     )()
@@ -246,7 +296,7 @@
         return carry
 
     lax.fori_loop(0, n_seq, fold, 0)
-    swap_all(
+    begin_swap(
         n_seq, seq, lambda s: mid.at[s], lambda s: got_b.at[s],
         lambda s: (s, opt), send_b, recv_b,
     )()
@@ -261,7 +311,7 @@
     stats[:, :cols] = jnp.sum(squares_raw, axis=0, keepdims=True)
     row_stat = row_ref[...]
     stats[:, cols:] = jnp.broadcast_to(jnp.sum(row_stat, axis=0, keepdims=True), (1, LANES))
-    swap_all(
+    begin_swap(
         n, me, lambda i: stats, lambda i: all_stats.at[i], any_device, send_c, recv_c
     )()
     all_stats[me] = stats[...]
@@ -275,7 +325,7 @@
     scaled = grad * factor
     moment = beta_one * code_ref[...].astype(f32) * scale_ref[...] + (1.0 - beta_one) * scaled
     peak[...] = jnp.max(jnp.abs(moment), axis=0, keepdims=True)
-    end_peaks = swap_all(
+    end_peaks = begin_swap(
         n, me, lambda i: peak, lambda i: all_peaks.at[i], any_device, send_d, recv_d
     )
     col_next = beta_two * col_ref[...] + (1.0 - beta_two) * (
@@ -329,8 +379,6 @@
     group = heads // n_seq
     own_rows = w_bc.shape[0]
 
-    w_all = lax.all_gather(w_bc.astype(bf16), ("seq", "opt"), axis=0, tiled=True)
-
     ones = (
         lax.broadcasted_iota(jnp.int32, (BLOCK, BLOCK), 0)
         <= lax.broadcasted_iota(jnp.int32, (BLOCK, BLOCK), 1)
@@ -351,20 +399,22 @@
     b_spec = pl.BlockSpec((length, state_dim), lambda h: (0, 0))
     c_spec = pl.BlockSpec((length, state_dim), lambda h: (0, 1))
     far_shape = (n_seq, 2, group, state_dim, head_dim)
-    square = heads * length * BLOCK
-
-    mixing = pl.pallas_call(
-        functools.partial(mixing_kernel, count),
+
+    w_shape = (own_rows, 2 * state_dim)
+    mixing, w_all = pl.pallas_call(
+        functools.partial(mixing_kernel, count, n_seq, n_opt),
         grid=(heads,),
-        in_specs=[tokens, tokens, run_spec],
-        out_specs=mix_spec,
-        out_shape=jax.ShapeDtypeStruct((count, BLOCK, BLOCK), f32),
-        compiler_params=params(),
-        cost_estimate=pl.CostEstimate(
-            flops=2 * square * head_dim * 10, bytes_accessed=4 * length * width, transcendentals=square
-        ),
-        name="mixing",
-    )(x, dy, running)
+        in_specs=[whole(), tokens, tokens, run_spec],
+        out_specs=[mix_spec, whole()],
+        out_shape=[
+            jax.ShapeDtypeStruct((count, BLOCK, BLOCK), f32),
+            jax.ShapeDtypeStruct((n_seq, n_opt) + w_shape, bf16),
+        ],
+        scratch_shapes=[pltpu.VMEM((n_opt, n_seq) + w_shape, bf16)] + dma(n_seq, n_opt),
+        compiler_params=params(collective_id=2, has_side_effects=True),
+        name="gather_and_mixing",
+    )(w_bc.astype(bf16), x, dy, running)
+    w_all = w_all.reshape(width, 2 * state_dim)
 
     proj = jnp.dot(layer_rows, w_all, preferred_element_type=f32).astype(bf16)
 
@@ -378,6 +428,7 @@
             jax.ShapeDtypeStruct((heads, count, state_dim, head_dim), bf16),
             jax.ShapeDtypeStruct((heads, count, state_dim, head_dim), bf16),
         ],
+        scratch_shapes=[pltpu.VMEM((state_dim, length), f32)] * 2,
         compiler_params=params(),
         name="local_states",
     )(x, dy, proj, proj, running)

time: 313 us -> 286 us (0.914)
  waiting for transfers between devices: 37.4 us -> 0 us
  Pallas kernels: 233 us -> 257 us
  between operations: 14.1 us -> 0.69 us
    all_gather x1 -> x0, waiting for transfers between devices: 37.3 us -> none  [per_device(): lax.all_gather(w_bc.astype(bf16), ('seq', 'opt'), axis=0, tiled=True)]
    pallas_call x1, Pallas kernels: 21.1 us -> 42.2 us  [per_device(): pl.pallas_call(functools.partial(mixing_kernel, count, n_seq, n_opt), gri...]
    pallas_call x1, Pallas kernels: 93.2 us -> 97.4 us  [per_device(): pl.pallas_call(functools.partial(carry_kernel, n_seq), in_specs=[whole(),...]
  transfers between devices with their start and end apart: 1 -> 0, of which waited for: 1 -> 0; matrix products, arithmetic and copies ran while one was open for 1% -> 0% of each run, Pallas kernels for 7% -> 0%
where the time goes in v2:
time: 286 us; the launch traced here: 284 us
  Pallas kernels  257 us (90%)
  local copies, waits for them, and re-layouts  14.3 us (5%)
  matrix products  8.62 us (3%)
  other arithmetic  3.48 us (1%)
    pallas_call x1, Pallas kernels, per_device(): pl.pallas_call(functools.partial(carry_kernel, n_seq), in_specs=[whole(),...  97.4 us
    pallas_call x1, Pallas kernels, per_device(): pl.pallas_call(functools.partial(step_kernel, n_seq, n_opt), in_specs=[wh...  66.2 us
    pallas_call x1, Pallas kernels, per_device(): pl.pallas_call(functools.partial(mixing_kernel, count, n_seq, n_opt), gri...  42.2 us
    pallas_call x1, Pallas kernels, per_device(): pl.pallas_call(functools.partial(grads_kernel, count), grid=(heads,), in_...  27.7 us
    pallas_call x1, Pallas kernels, per_device(): pl.pallas_call(functools.partial(local_kernel, count), grid=(heads,), in_...  23.3 us

profile of v2, /device:TPU:0, one launch (start us, length us, event | category | flops | bytes accessed | tf_op | source)
XLA Modules:
  0.0 283.8 jit_solution(8944640571909554380)
XLA Ops:
  0.6 0.9 reshape_squeeze.3
  1.5 0.2 convolution_bitcast_fusion
  1.7 0.7 reshape.32.run_ref
  2.4 1.5 convert_element_type.15.w_ref
  3.9 42.2 %gather_and_mixing.1 = (f32[2,256,256]{2,1,0:T(8,128)}, bf16[8,4,128,256]{3,2,1,0:T(8,128)(2,1)}) custom-call(bf16[128,256]{1,0:T(8,128)(2,1)} %convert_element_type.15.w_ref, bf16[512,4096]{1,0:T(8,128)(2,1)} %bitcast.31, bf16[512,4096]{1,0:T(8,128)(2,1)} %bitcast.34, f32[32,2,256]{2,1,0:T(2,128)} %reshape.32.run_ref), custom_call_target="tpu_custom_call" | custom-call | tf_op jit(solution)/shard_map/gather_and_mixing/pallas_call | solution.py:404
  46.1 4.9 %fusion.7.b_ref.c_ref = bf16[512,256]{1,0:T(8,128)(2,1)} fusion(bf16[4096,256]{1,0:T(8,128)(2,1)} %bitcast.45, bf16[1,512,4096]{2,1,0:T(8,128)(2,1)} %param.10), kind=kOutput, calls=%fused_computation.7 | convolution fusion | flops 1073872896 | bytes 6553600 | tf_op jit(solution)/shard_map/dot_general | solution.py:419
  50.9 0.0 copy-start
  50.9 23.3 %local_states.1 = (bf16[8,2,4,128,128]{4,3,2,1,0:T(8,128)(2,1)}, bf16[32,2,128,128]{3,2,1,0:T(8,128)(2,1)}, bf16[32,2,128,128]{3,2,1,0:T(8,128)(2,1)}) custom-call(bf16[512,4096]{1,0:T(8,128)(2,1)} %bitcast.32, bf16[512,4096]{1,0:T(8,128)(2,1)} %bitcast.35, bf16[512,256]{1,0:T(8,128)(2,1)} %fusion.7.b_ref.c_ref, bf16[512,256]{1,0:T(8,128)(2,1)} %fusion.7.b_ref.c_ref, ...), custom_call_target="tpu_custom_call" | custom-call | tf_op jit(solution)/shard_map/local_states/pallas_call | solution.py:421
  74.2 0.0 copy-done
  74.2 0.5 slice_reduce_fusion
  74.7 0.1 exp.11
  74.8 0.7 broadcast_in_dim.18.decay_ref
  75.5 97.4 %carry_states.1.far_ref = bf16[8,2,4,128,128]{4,3,2,1,0:T(8,128)(2,1)} custom-call(bf16[8,2,4,128,128]{4,3,2,1,0:T(8,128)(2,1)} %get-tuple-element.21.send_ref, f32[8,4,1,128]{3,2,1,0:T(1,128)} %broadcast_in_dim.18.decay_ref), custom_call_target="tpu_custom_call" | custom-call | tf_op jit(solution)/shard_map/carry_states/pallas_call | solution.py:436
  172.9 27.7 %grads.1 = (bf16[512,4096]{1,0:T(8,128)(2,1)}, bf16[512,256]{1,0:T(8,128)(2,1)}) custom-call(f32[32]{0:T(128)} %skip_ref.1, bf16[512,4096]{1,0:T(8,128)(2,1)} %bitcast.33, bf16[512,4096]{1,0:T(8,128)(2,1)} %bitcast.36, bf16[512,256]{1,0:T(8,128)(2,1)} %fusion.7.b_ref.c_ref, bf16[512,256]{1,0:T(8,128)(2,1)} %fusion.7.b_ref.c_ref, ...), custom_call_target="tpu_custom_call" | custom-call | tf_op jit(solution)/shard_map/grads/pallas_call | solution.py:453
  200.6 3.6 %fusion = bf16[4096,256]{0,1:T(8,128)(2,1)S(1)} fusion(bf16[512,256]{1,0:T(8,128)(2,1)} %get-tuple-element.24, bf16[1,512,4096]{2,1,0:T(8,128)(2,1)} %param.10), kind=kOutput, calls=%fused_computation.1 | convolution fusion | flops 1074790400 | bytes 6553600 | tf_op jit(solution)/shard_map/dot_general | solution.py:475
  204.2 2.5 copy.19
  206.7 0.0 copy-start.1
  206.7 3.2 %copy.24 = bf16[8,4,128,256]{3,2,0,1:T(8,128)(2,1)} copy(bf16[8,4,128,256]{3,2,1,0:T(8,128)(2,1)} %bitcast.38) | data formatting | bytes 4194304 | tf_op jit(solution)/shard_map/reshape | solution.py:478
  209.9 0.0 copy-done.1
  209.9 0.7 copy.21.row_ref
  210.6 66.2 %sum_and_step.1 = (f32[128,256]{1,0:T(8,128)}, bf16[128,256]{1,0:T(8,128)(2,1)}, f32[1,256]{1,0:T(1,128)}, f32[128,1]{1,0:T(8,128)}, f32[1,256]{1,0:T(1,128)}) custom-call(bf16[4,8,128,256]{3,2,1,0:T(8,128)(2,1)} %bitcast.37, f32[128,256]{1,0:T(8,128)} %w_ref.1, bf16[128,256]{1,0:T(8,128)(2,1)} %code_ref.1, f32[1,256]{1,0:T(1,128)} %bitcast.39, ...), custom_call_target="tpu_custom_call" | custom-call | tf_op jit(solution)/shard_map/sum_and_step/pallas_call | solution.py:481
  276.8 1.5 reduce.1
  278.3 1.6 copy.29
  279.9 1.5 copy.30
  281.4 1.2 copy.31
  282.6 1.2 copy.32
  (1 shorter events, 0.0 us)
Async XLA Ops:
  50.9 23.3 %copy-start = (f32[32,2,256]{2,1,0:T(2,128)S(1)}, f32[32,2,256]{2,1,0:T(2,128)}, u32[]{:S(2)}) copy-start(f32[32,2,256]{2,1,0:T(2,128)} %reshape.32.run_ref) | copy-start | bytes 196612
  206.7 3.2 %copy-start.1 = (f32[128]{0:T(128)S(1)}, f32[128]{0:T(128)}, u32[]{:S(2)}) copy-start(f32[128]{0:T(128)} %param.18) | copy-start | bytes 1540
